TPU v7x, 32 devices: a whole 2x2x4 slice. The times are simulated.
32 devices in a mesh: dp: 1, vocab: 32 (over z, y, x, core).
Axes of the slice: x: 2, y: 2, z: 4, core: 2. Of those that a mesh axis runs over, the one named last changes fastest.
Arguments:
- input_ids: int32 [256], P('dp'), may hold values from 0 to 63999
- target_ids: int32 [256], P('dp'), may hold values from 0 to 63999
- loss_mask: int32 [256], P('dp'), may hold values 0 or 1
- final_hidden: bfloat16 [256, 3584], P('dp'), may hold values from -5 to 5, as said below
- norm_gain: float32 [3584], replicated, may hold values from 0.25 to 1.75
- embed_cotangent: bfloat16 [256, 3584], P('dp'), may hold values from -0.059814453 to 0.059814453
- table: bfloat16 [64000, 3584], P(('dp', 'vocab')), may hold values from -0.08351914 to 0.08351914, as said below
Outputs:
- embedded: bfloat16 [256, 3584], P('dp')
- loss: float32 [], replicated
- grad_hidden: bfloat16 [256, 3584], P('dp')
- gain_grad: float32 [3584], replicated
- table_grad: bfloat16 [64000, 3584], P(('dp', 'vocab'))
Inputs may be any that keep to these rules, and one draw needn't show every extreme that they name: Every entry of table lies within -5 / sqrt(3584) and 5 / sqrt(3584). Every entry of final_hidden lies within -5 and 5.
All inputs are finite; a program needn't handle non-finite values.
Results may differ from a plain program's by a relative error of at most 0.003.
Values may be sent and summed in bfloat16 or wider, within the bound.
A program may use at most 256 MiB of HBM per device.

v0:
```python
import math
import jax
import jax.numpy as jnp
from jax import lax
from jax.sharding import PartitionSpec as P

SOFTCAP = 30
EPSILON = 1e-06


def norm_backward(upstream, widened, inv_rms, norm_gain):
    scaled_up = upstream * norm_gain
    mean_dot = jnp.mean(scaled_up * widened, axis=1, keepdims=True)
    gradient = inv_rms * scaled_up - widened * (inv_rms * inv_rms * inv_rms) * mean_dot
    gain_part = jnp.sum(upstream * widened * inv_rms, axis=0)
    return (gradient.astype(jnp.bfloat16), gain_part)


def body(input_ids, target_ids, loss_mask, final_hidden, norm_gain, embed_cotangent, table):
    row_count = table.shape[0]
    embed_scale = math.sqrt(table.shape[1])
    owner = lax.axis_index(("dp", "vocab"))
    first_row = owner * row_count
    every_id, every_target, every_mask = (
        lax.all_gather(input_ids, "dp", axis=0, tiled=True),
        lax.all_gather(target_ids, "dp", axis=0, tiled=True),
        lax.all_gather(loss_mask, "dp", axis=0, tiled=True),
    )
    token_total = every_id.shape[0]
    per_group = token_total // lax.axis_size("dp")
    share_rows = token_total // lax.axis_size(("dp", "vocab"))
    widened = final_hidden.astype(jnp.float32)
    inv_rms = lax.rsqrt(jnp.mean(widened * widened, axis=1, keepdims=True) + EPSILON)
    normed = (widened * inv_rms * norm_gain).astype(jnp.bfloat16)
    normed_all, cotangent_all = (
        lax.all_gather(normed, "dp", axis=0, tiled=True),
        lax.all_gather(embed_cotangent, "dp", axis=0, tiled=True),
    )

    def lookup_term():
        wanted = lax.slice_in_dim(every_id, 0, per_group * lax.axis_size("dp"), axis=0) - first_row
        inside = (wanted >= 0) & (wanted < row_count)
        picked = jnp.take(table, jnp.clip(wanted, 0, row_count - 1), axis=0)
        return jnp.where(inside[:, None], picked.astype(jnp.float32), 0.0)

    group_rows = lax.psum_scatter(
        lookup_term().astype(jnp.bfloat16), "dp", scatter_dimension=0, tiled=True
    ).astype(jnp.float32)
    found = lax.psum(group_rows.astype(jnp.bfloat16), "vocab").astype(jnp.float32)
    embedded = (found * embed_scale).astype(jnp.bfloat16)
    raw_logits = lax.dot_general(
        normed_all, table, (((1,), (1,)), ((), ())), preferred_element_type=jnp.float32
    )
    capped = SOFTCAP * jnp.tanh(raw_logits / SOFTCAP)
    exp_logits = jnp.exp(capped)
    local_targets = every_target - first_row
    target_hit = lax.broadcasted_iota(jnp.int32, capped.shape, 1) == local_targets[:, None]
    token_weight = every_mask.astype(jnp.float32)
    picked_sum = jnp.sum(token_weight * jnp.sum(jnp.where(target_hit, capped, 0.0), axis=1))
    sum_exp, target_sum = lax.psum((jnp.sum(exp_logits, axis=1), picked_sum), ("dp", "vocab"))
    loss = (jnp.sum(token_weight * jnp.log(sum_exp)) - target_sum) / jnp.maximum(
        jnp.sum(token_weight), 1.0
    )
    slope = (
        token_weight[:, None]
        * (exp_logits / sum_exp[:, None] - target_hit.astype(jnp.float32))
        * (1.0 - (capped / SOFTCAP) ** 2)
    )
    slope_low = slope.astype(jnp.bfloat16)
    head_part = lax.dot_general(
        slope_low, normed_all, (((0,), (0,)), ((), ())), preferred_element_type=jnp.float32
    )
    local_ids = every_id - first_row
    owned = (local_ids >= 0) & (local_ids < row_count)
    segment_ids = jnp.where(owned, local_ids, row_count)
    embed_part = (
        jax.ops.segment_sum(
            cotangent_all.astype(jnp.float32), segment_ids, num_segments=row_count + 1
        )[:row_count]
        * embed_scale
    )
    table_grad = (head_part + embed_part).astype(jnp.bfloat16)

    def upstream_term():
        block = lax.slice_in_dim(slope_low, 0, share_rows * lax.axis_size(("dp", "vocab")), axis=0)
        return jnp.dot(block, table, preferred_element_type=jnp.float32)

    upstream = lax.psum_scatter(upstream_term(), ("dp", "vocab"), scatter_dimension=0, tiled=True)
    offset_rows = lax.axis_index("vocab") * share_rows
    widened_share = lax.dynamic_slice_in_dim(widened, offset_rows, share_rows, 0)
    inv_share = lax.dynamic_slice_in_dim(inv_rms, offset_rows, share_rows, 0)
    gradient_share, gain_part = norm_backward(upstream, widened_share, inv_share, norm_gain)
    gain_grad = lax.psum(gain_part, ("dp", "vocab"))
    grad_hidden = lax.all_gather(gradient_share, "vocab", axis=0, tiled=True)
    return (embedded, loss, grad_hidden, gain_grad, table_grad)


def solution(mesh):
    placed = (
        P("dp"),
        P("dp"),
        P("dp"),
        P("dp", None),
        P(),
        P("dp", None),
        P(("dp", "vocab"), None),
    )
    return jax.shard_map(
        body,
        mesh=mesh,
        in_specs=placed,
        out_specs=(P("dp", None), P(), P("dp", None), P(), P(("dp", "vocab"), None)),
        check_vma=False,
    )
```

profile of v0, /device:TPU:0, one launch (start us, length us, event | category | flops | bytes accessed | tf_op | source)
XLA Modules:
  0.0 414.2 jit_solution(4255250760945379497)
XLA Ops:
  7.2 0.0 reduce-scatter.2.cloned.1.call-start
  7.2 1.9 multiply_reduce_fusion
  9.2 0.7 broadcast_subtract_fusion
  9.9 8.1 %select_reduce_fusion = (f32[256]{0:T(256)S(1)}, f32[256]{0:T(256)S(1)}, f32[256,2000]{0,1:T(8,128)S(1)}) fusion(s32[256]{0:T(256)S(1)} %broadcast_subtract_fusion, bf16[2000,3584]{1,0:T(8,128)(2,1)} %param.13, f32[3584]{0:T(1024)} %param.11, f32[256]{0:T(256)S(1)} %add_rsqrt_fusion, bf16[256,3584]{1,0:T(8,128)(2,1)} %param.10), kind=kOutput, calls=%fused_computation.15 | convolution fusion | flops 3676757504 | bytes 18237440 | tf_op jit(solution)/shard_map/dot_general | solution.py:51
  18.0 42.0 %psum.29 = f32[256]{0:T(256)S(1)} all-reduce(f32[256]{0:T(256)S(1)} %get-tuple-element.8), channel_id=1, replica_groups=mesh['dp'=1,'vocab'=32] {'dp','vocab'}, use_global_device_ids=true, to_apply=%region_3.4 | all-reduce | flops 256 | bytes 2048 | tf_op jit(solution)/shard_map/psum | solution.py:60
  60.0 9.4 %fusion.7 = f32[256,3584]{1,0:T(8,128)} fusion(bf16[2000,3584]{1,0:T(8,128)(2,1)} %param.13, f32[256,2000]{0,1:T(8,128)S(1)} %get-tuple-element.19, f32[256]{0:T(256)S(1)} %psum.29, f32[256]{0:T(256)S(1)} %convert_element_type.42, s32[256]{0:T(256)S(1)} %broadcast_subtract_fusion), kind=kOutput, calls=%fused_computation.34 | convolution fusion | flops 3675136000 | bytes 20057088 | tf_op jit(solution)/shard_map/dot_general | solution.py:86
  69.4 0.0 all-reduce.3.cloned.1.call-start
  69.4 0.6 copy-done.3
  70.0 11.7 %gather_fusion = bf16[256,3584]{1,0:T(8,128)(2,1)} fusion(bf16[2000,3584]{1,0:T(8,128)(2,1)} %param.13, s32[1024]{0:T(1024)S(1)} %pad_clamp_fusion), kind=kCustom, calls=%fused_computation | custom fusion | bytes 3671040 | tf_op jit(solution)/shard_map/jit(_take)/gather | solution.py:43
  81.7 3.9 select_convert_fusion
  85.6 0.2 all-gather.2.cloned.1.call-start
  85.9 2.2 convert_element_type.43
  88.1 0.1 fusion.6
  88.2 0.6 convert_reduce_fusion
  89.5 121.3 %reduce-scatter.2.cloned.1.call-done = f32[8,3584]{1,0:T(8,128)} async-done(((f32[256,3584]{1,0:T(8,128)}), f32[8,3584]{1,0:T(8,128)}) %reduce-scatter.2.cloned.1.call-update) | async-done | bytes 114704 | tf_op jit(solution)/shard_map/reduce_scatter | solution.py:88
  210.7 1.2 multiply_reduce_fusion.1
  211.9 1.7 subtract_convert_fusion
  213.6 18.1 %scatter_custom_fusion = f32[2001,3584]{1,0:T(8,128)} fusion(s32[256]{0:T(256)S(1)} %subtract_select_fusion, f32[]{:T(128)} %constant.21.clone.1, bf16[256,3584]{1,0:T(8,128)(2,1)} %param.12), kind=kCustom, calls=%fused_computation.5 | custom fusion | flops 1835008 | bytes 30521348 | tf_op jit(solution)/shard_map/scatter-add | solution.py:77
  231.7 17.1 %fusion.1 = bf16[2000,3584]{1,0:T(8,128)(2,1)} fusion(f32[2001,3584]{1,0:T(8,128)} %scatter_custom_fusion, f32[3584]{0:T(1024)S(1)} %copy-done.2, f32[256]{0:T(256)S(1)} %add_rsqrt_fusion, bf16[256,3584]{1,0:T(8,128)(2,1)S(1)} %copy-done, f32[256,2000]{0,1:T(8,128)} %copy-done.1, f32[256]{0:T(256)S(1)} %psum.29, f32[256]{0:T(256)S(1)} %convert_element_type.42, ...), kind=kOutput, calls=%fused_computation.4 | convolution fusion | flops 3700310016 | bytes 46909440 | tf_op jit(solution)/shard_map/dot_general | solution.py:70
  248.8 97.3 %all-reduce.3.cloned.1.call-done = bf16[256,3584]{1,0:T(8,128)(2,1)} async-done(((bf16[256,3584]{1,0:T(8,128)(2,1)}), bf16[256,3584]{1,0:T(8,128)(2,1)}) %all-reduce.3.cloned.1.call-update) | async-done | bytes 1835024 | tf_op jit(solution)/shard_map/psum | solution.py:49
  346.2 3.0 multiply_convert_fusion.1
  349.2 39.6 %all-reduce = (f32[]{:T(128)}, f32[3584]{0:T(1024)}) all-reduce(f32[]{:T(128)} %get-tuple-element.11, f32[3584]{0:T(1024)S(1)} %get-tuple-element.5), channel_id=1, replica_groups=mesh['dp'=1,'vocab'=32] {'dp','vocab'}, use_global_device_ids=true, to_apply=%region_7.8 | all-reduce | flops 3585 | bytes 28680 | tf_op jit(solution)/shard_map/psum | solution.py:60
  390.1 13.7 %all-gather.2.cloned.1.call-done = bf16[256,3584]{1,0:T(8,128)(2,1)} async-done(((bf16[8,3584]{1,0:T(8,128)(2,1)}), bf16[256,3584]{1,0:T(8,128)(2,1)}) %all-gather.2.cloned.1.call-update) | async-done | bytes 1835024 | tf_op jit(solution)/shard_map/all_gather | solution.py:94
  403.7 2.8 copy.14
  (18 shorter events, 0.1 us)
Async XLA Ops:
  7.2 203.6 %reduce-scatter.2.cloned.1.call-start = ((), (), s32[]{:S(2)}) async-start(), calls=%async_computation.2 | async-start | bytes 3784704 | tf_op jit(solution)/shard_map/reduce_scatter | solution.py:88
  9.9 50.1 %copy-start.4 = (s32[256]{0:T(256)S(1)}, s32[256]{0:T(256)}, u32[]{:S(2)}) copy-start(s32[256]{0:T(256)} %param.9) | copy-start | bytes 3076
  18.0 51.4 %copy-start.1 = (f32[256,2000]{0,1:T(8,128)}, f32[256,2000]{0,1:T(8,128)S(1)}, u32[]{:S(2)}) copy-start(f32[256,2000]{0,1:T(8,128)S(1)} %get-tuple-element.19) | copy-start | bytes 6144004
  69.3 0.7 copy-start.3
  69.4 276.8 %all-reduce.3.cloned.1.call-start = ((), (), s32[]{:S(2)}) async-start(), calls=%async_computation.1 | async-start | bytes 3670016 | tf_op jit(solution)/shard_map/psum | solution.py:49
  81.7 4.1 copy-start
  85.6 125.1 %copy-start.2 = (f32[3584]{0:T(1024)S(1)}, f32[3584]{0:T(1024)}, u32[]{:S(2)}) copy-start(f32[3584]{0:T(1024)} %param.11) | copy-start | bytes 43012
  85.6 318.1 %all-gather.2.cloned.1.call-start = ((), (), s32[]{:S(2)}) async-start(), calls=%async_computation.3 | async-start | bytes 1892352 | tf_op jit(solution)/shard_map/all_gather | solution.py:94
Sparse Core Ops, SparseCore 0:
  69.5 141.1 reduce-scatter.1
  216.6 129.4 all-reduce.2
  349.0 54.6 all-gather.1
where the time goes:
time: 415 us; the launch traced here: 414 us
  waiting for transfers between devices  232 us (56%)
  blocking collectives  81.6 us (20%)
  matrix products  34.6 us (8%)
  other arithmetic  33.4 us (8%)
  between operations  16.9 us (4%)
  local copies, waits for them, and re-layouts  15.1 us (4%)
    reduce_scatter x1, waiting for transfers between devices, body(): lax.psum_scatter(upstream_term(), ('dp', 'vocab'), scatter_dimension=0, t...  121 us
    psum x1, waiting for transfers between devices, body(): lax.psum(group_rows.astype(jnp.bfloat16), 'vocab').astype(jnp.float32)  97.3 us
    psum x2, blocking collectives, body(): lax.psum((jnp.sum(exp_logits, axis=1), picked_sum), ('dp', 'vocab'))  81.6 us
    scatter-add x1, other arithmetic, body(): jax.ops.segment_sum(cotangent_all.astype(jnp.float32), segment_ids, num_s...  18.1 us
    dot_general x1, matrix products, body(): lax.dot_general(slope_low, normed_all, (((0,), (0,)), ((), ())), preferre...  17.1 us
    all_gather x1, waiting for transfers between devices, body(): grad_hidden = lax.all_gather(gradient_share, 'vocab', axis=0, tiled=True)  13.7 us
    gather x1, local copies, waits for them, and re-layouts, lookup_term(): picked = jnp.take(table, jnp.clip(wanted, 0, row_count - 1), axis=0)  11.7 us
    dot_general x1, matrix products, upstream_term(): return jnp.dot(block, table, preferred_element_type=jnp.float32)  9.38 us
  transfers between devices with their start and end apart: 3, of which 3 were waited for; matrix products, arithmetic and copies ran while one was open for 14% of the time, Pallas kernels for 0%

commit v1 on v0

--- a/solution.py
+++ b/solution.py
@@ -46,7 +46,9 @@
     group_rows = lax.psum_scatter(
         lookup_term().astype(jnp.bfloat16), "dp", scatter_dimension=0, tiled=True
     ).astype(jnp.float32)
-    found = lax.psum(group_rows.astype(jnp.bfloat16), "vocab").astype(jnp.float32)
+    found = jnp.sum(lax.all_gather(group_rows.astype(jnp.bfloat16), "vocab"), axis=0).astype(
+        jnp.float32
+    )
     embedded = (found * embed_scale).astype(jnp.bfloat16)
     raw_logits = lax.dot_general(
         normed_all, table, (((1,), (1,)), ((), ())), preferred_element_type=jnp.float32

time: 415 us -> 620 us (1.49)
  waiting for transfers between devices: 232 us -> 413 us
  other arithmetic: 33.4 us -> 51 us
    all_gather x0 -> x1, waiting for transfers between devices: none -> 276 us  [body(): lax.all_gather(group_rows.astype(jnp.bfloat16), 'vocab')]
    psum x1 -> x0, waiting for transfers between devices: 97.3 us -> none  [body(): lax.psum(group_rows.astype(jnp.bfloat16), 'vocab').astype(jnp.float32)]
    reduce_sum x0 -> x1, other arithmetic: none -> 19.2 us  [body(): jnp.sum(lax.all_gather(group_rows.astype(jnp.bfloat16), 'vocab'), axis=0)]
    reduce_scatter x1, waiting for transfers between devices: 121 us -> 137 us  [body(): lax.psum_scatter(upstream_term(), ('dp', 'vocab'), scatter_dimension=0, t...]
    all_gather x1, waiting for transfers between devices: 13.7 us -> 0.02 us  [body(): grad_hidden = lax.all_gather(gradient_share, 'vocab', axis=0, tiled=True)]
  transfers between devices with their start and end apart: 3 -> 3, of which waited for: 3 -> 2; matrix products, arithmetic and copies ran while one was open for 14% -> 9% of each run, Pallas kernels for 0% -> 0%
where the time goes in v1:
time: 620 us
  waiting for transfers between devices  413 us (67%)
  blocking collectives  82.8 us (13%)
  other arithmetic  51 us (8%)
  matrix products  40.6 us (7%)
  between operations  16.9 us (3%)
  local copies, waits for them, and re-layouts  14.9 us (2%)
    all_gather x1, waiting for transfers between devices, body(): lax.all_gather(group_rows.astype(jnp.bfloat16), 'vocab')  276 us
    reduce_scatter x1, waiting for transfers between devices, body(): lax.psum_scatter(upstream_term(), ('dp', 'vocab'), scatter_dimension=0, t...  137 us
    psum x2, blocking collectives, body(): lax.psum((jnp.sum(exp_logits, axis=1), picked_sum), ('dp', 'vocab'))  82.8 us
    reduce_sum x1, other arithmetic, body(): jnp.sum(lax.all_gather(group_rows.astype(jnp.bfloat16), 'vocab'), axis=0)  19.2 us
    scatter-add x1, other arithmetic, body(): jax.ops.segment_sum(cotangent_all.astype(jnp.float32), segment_ids, num_s...  18 us
    dot_general x1, matrix products, body(): lax.dot_general(slope_low, normed_all, (((0,), (0,)), ((), ())), preferre...  17.3 us
  transfers between devices with their start and end apart: 3, of which 2 were waited for; matrix products, arithmetic and copies ran while one was open for 9% of the time, Pallas kernels for 0%

profile of v1, /device:TPU:0, one launch (start us, length us, event | category | flops | bytes accessed | tf_op | source)
XLA Modules:
  0.0 619.9 jit_solution(6515225682340192654)
XLA Ops:
  7.2 1.9 multiply_reduce_fusion
  9.2 0.7 broadcast_subtract_fusion
  9.9 11.6 %select_reduce_fusion = (f32[256]{0:T(256)S(1)}, f32[256]{0:T(256)S(1)}, f32[256,2000]{0,1:T(8,128)}) fusion(s32[256]{0:T(256)S(1)} %broadcast_subtract_fusion, bf16[2000,3584]{1,0:T(8,128)(2,1)} %param.13, f32[3584]{0:T(1024)} %param.11, f32[256]{0:T(256)S(1)} %add_rsqrt_fusion, bf16[256,3584]{1,0:T(8,128)(2,1)} %param.10), kind=kOutput, calls=%fused_computation.15 | convolution fusion | flops 3676757504 | bytes 18237440 | tf_op jit(solution)/shard_map/dot_general | solution.py:53
  21.4 41.9 %psum.21 = f32[256]{0:T(256)S(1)} all-reduce(f32[256]{0:T(256)S(1)} %get-tuple-element.8), channel_id=1, replica_groups=mesh['dp'=1,'vocab'=32] {'dp','vocab'}, use_global_device_ids=true, to_apply=%region_3.4 | all-reduce | flops 256 | bytes 2048 | tf_op jit(solution)/shard_map/psum | solution.py:62
  63.3 11.7 %fusion.7 = f32[256,3584]{1,0:T(8,128)} fusion(bf16[2000,3584]{1,0:T(8,128)(2,1)} %param.13, f32[256,2000]{0,1:T(8,128)} %get-tuple-element.19, f32[256]{0:T(256)S(1)} %psum.21, f32[256]{0:T(256)S(1)} %convert_element_type.58, s32[256]{0:T(256)S(1)} %broadcast_subtract_fusion), kind=kOutput, calls=%fused_computation.35 | convolution fusion | flops 3675136000 | bytes 20057088 | tf_op jit(solution)/shard_map/dot_general | solution.py:88
  75.1 0.0 all-gather.5.cloned.1.call-start
  75.2 1.4 copy-done
  76.6 2.2 convert_element_type.59
  78.8 0.1 fusion.6
  78.9 137.4 %reduce-scatter.2.cloned.1.call-done = f32[8,3584]{1,0:T(8,128)} async-done(((f32[256,3584]{1,0:T(8,128)}), f32[8,3584]{1,0:T(8,128)}) %reduce-scatter.2.cloned.1.call-update) | async-done | bytes 114704 | tf_op jit(solution)/shard_map/reduce_scatter | solution.py:90
  216.3 1.2 multiply_reduce_fusion.1
  217.4 1.7 subtract_convert_fusion
  219.1 0.2 all-gather.3.cloned.1.call-start
  219.4 11.7 %gather_fusion = bf16[256,3584]{1,0:T(8,128)(2,1)} fusion(bf16[2000,3584]{1,0:T(8,128)(2,1)} %param.13, s32[1024]{0:T(1024)S(1)} %pad_clamp_fusion), kind=kCustom, calls=%fused_computation | custom fusion | bytes 3671040 | tf_op jit(solution)/shard_map/jit(_take)/gather | solution.py:43
  231.1 3.7 select_convert_fusion
  234.9 0.7 convert_reduce_fusion
  236.2 18.0 %scatter_custom_fusion = f32[2001,3584]{1,0:T(8,128)} fusion(s32[256]{0:T(256)S(1)} %subtract_select_fusion, f32[]{:T(128)} %constant.22.clone.1, bf16[256,3584]{1,0:T(8,128)(2,1)} %param.12), kind=kCustom, calls=%fused_computation.5 | custom fusion | flops 1835008 | bytes 30521348 | tf_op jit(solution)/shard_map/scatter-add | solution.py:79
  254.3 17.3 %fusion.1 = bf16[2000,3584]{1,0:T(8,128)(2,1)} fusion(f32[2001,3584]{1,0:T(8,128)} %scatter_custom_fusion, f32[3584]{0:T(1024)S(1)} %copy-done.2, f32[256]{0:T(256)S(1)} %add_rsqrt_fusion, bf16[256,3584]{1,0:T(8,128)(2,1)S(1)} %copy-done, f32[256,2000]{0,1:T(8,128)} %get-tuple-element.19, f32[256]{0:T(256)S(1)} %psum.21, f32[256]{0:T(256)S(1)} %convert_element_type.58, ...), kind=kOutput, calls=%fused_computation.4 | convolution fusion | flops 3700310016 | bytes 46909440 | tf_op jit(solution)/shard_map/dot_general | solution.py:72
  271.6 40.9 %all-reduce = (f32[]{:T(128)}, f32[3584]{0:T(1024)}) all-reduce(f32[]{:T(128)} %get-tuple-element.11, f32[3584]{0:T(1024)S(1)} %get-tuple-element.5), channel_id=1, replica_groups=mesh['dp'=1,'vocab'=32] {'dp','vocab'}, use_global_device_ids=true, to_apply=%region_7.8 | all-reduce | flops 3585 | bytes 28680 | tf_op jit(solution)/shard_map/psum | solution.py:62
  313.8 275.9 %all-gather.3.cloned.1.call-done = bf16[32,256,3584]{2,1,0:T(8,128)(2,1)} async-done(((bf16[1,256,3584]{2,1,0:T(8,128)(2,1)}), bf16[32,256,3584]{2,1,0:T(8,128)(2,1)}) %all-gather.3.cloned.1.call-update) | async-done | bytes 58720272 | tf_op jit(solution)/shard_map/all_gather | solution.py:49
  589.7 19.2 %reduce_sum.84 = bf16[256,3584]{1,0:T(8,128)(2,1)S(1)} reduce(bf16[32,256,3584]{2,1,0:T(8,128)(2,1)} %all-gather.3.cloned.1.call-done, bf16[]{:T(256)} %constant.23.clone.1), dimensions={0}, to_apply=%region_0.0 | reduce | flops 28442624 | bytes 60555264 | tf_op jit(solution)/shard_map/reduce_sum | solution.py:49
  608.9 1.5 multiply_convert_fusion.1
  610.5 0.5 copy-done.1
  611.0 1.2 copy.13
  (19 shorter events, 0.2 us)
Async XLA Ops:
  7.2 209.1 %reduce-scatter.2.cloned.1.call-start = ((), (), s32[]{:S(2)}) async-start(), calls=%async_computation.2 | async-start | bytes 3784704 | tf_op jit(solution)/shard_map/reduce_scatter | solution.py:90
  9.9 53.5 %copy-start.4 = (s32[256]{0:T(256)S(1)}, s32[256]{0:T(256)}, u32[]{:S(2)}) copy-start(s32[256]{0:T(256)} %param.9) | copy-start | bytes 3076
  75.1 1.5 copy-start
  75.1 141.2 %copy-start.2 = (f32[3584]{0:T(1024)S(1)}, f32[3584]{0:T(1024)}, u32[]{:S(2)}) copy-start(f32[3584]{0:T(1024)} %param.11) | copy-start | bytes 43012
  75.1 144.3 %copy-start.3 = (s32[256]{0:T(256)S(1)}, s32[256]{0:T(256)}, u32[]{:S(2)}) copy-start(s32[256]{0:T(256)} %param.7) | copy-start | bytes 3076
  75.1 238.7 %all-gather.5.cloned.1.call-start = ((), (), s32[]{:S(2)}) async-start(), calls=%async_computation.3 | async-start | bytes 1892352 | tf_op jit(solution)/shard_map/all_gather | solution.py:96
  219.1 370.6 %all-gather.3.cloned.1.call-start = ((), (), s32[]{:S(2)}) async-start(), calls=%async_computation.1 | async-start | bytes 60555264 | tf_op jit(solution)/shard_map/all_gather | solution.py:49
  608.9 2.1 copy-start.1
Sparse Core Ops, SparseCore 0:
  75.2 140.9 reduce-scatter.1
  219.7 51.5 all-gather.4
  274.7 314.9 all-gather.2
